TPU v7x, 32 devices: a whole 2x2x4 slice. The times are simulated.
32 devices in a mesh: dp: 8 (over y, x, core), expert: 4 (over z).
Axes of the slice: x: 2, y: 2, z: 4, core: 2. Of those that a mesh axis runs over, the one named last changes fastest.
Arguments:
- hidden_states: bfloat16 [4, 8192, 4096], P(None, ('dp', 'expert')), may hold values from -8 to 8
- router_weight: bfloat16 [4, 8, 4096], replicated, may hold values from -0.125 to 0.125
- expert_ids: int32 [4, 8192, 2], P(None, ('dp', 'expert')), may hold values from 0 to 7, as said below
Outputs:
- router_grad: float32 [4, 8, 4096], P(None, None, 'dp')
- losses: float32 [4, 2], replicated
Inputs may be any that keep to these rules, and one draw needn't show every extreme that they name: `expert_ids`: each token names 2 different experts in each layer.
All inputs are finite; a program needn't handle non-finite values.
Results may differ from a plain program's by a relative error of at most 0.0018.
Values sent between devices are 32-bit elements; how exact they have to be, the bound alone decides.
A program may use at most 64 MiB of HBM per device.

v0:
```python
import jax
import jax.numpy as jnp
from jax import lax
from jax.sharding import PartitionSpec as P

balance_coef = 0.02
zloss_coef = 0.001


def local_counts(chosen, experts):
    labels = jnp.arange(experts, dtype=jnp.int32)[:, None]
    counts = jnp.zeros((experts,), jnp.float32)
    for slot in range(chosen.shape[1]):
        counts = counts + jnp.sum((chosen[:, slot][None, :] == labels).astype(jnp.float32), axis=1)
    return counts


def on_device(hidden_states, router_weight, expert_ids):
    layers = hidden_states.shape[0]
    rows = hidden_states.shape[1]
    experts = router_weight.shape[1]
    picks = expert_ids.shape[2]
    tokens_all = rows * lax.axis_size("dp") * lax.axis_size("expert")
    terms = []
    count_list = []
    prob_sums = []
    square_sums = []
    for layer in range(layers):
        states = hidden_states[layer]
        logits = lax.dot_general(
            router_weight[layer],
            states,
            (((1,), (1,)), ((), ())),
            preferred_element_type=jnp.float32,
        )
        expo = jnp.exp(logits)
        total = jnp.sum(expo, axis=0)
        probs = expo / total[None, :]
        lse = jnp.log(total)
        prob_sums.append(jnp.sum(probs, axis=1))
        square_sums.append(jnp.sum(lse * lse))
        counts = lax.psum(local_counts(expert_ids[layer], experts), ("dp", "expert"))
        count_list.append(counts)
        share = counts / (tokens_all * picks)
        pull = balance_coef * experts * share
        mixed = jnp.sum(probs * pull[:, None], axis=0)
        dlogits = probs * (pull[:, None] - mixed[None, :]) + 2.0 * zloss_coef * lse[None, :] * probs
        dlogits = dlogits.astype(jnp.bfloat16)
        term = jnp.dot(dlogits, states, preferred_element_type=jnp.float32)
        terms.append(term)
    columns = lax.psum_scatter(jnp.stack(terms), "dp", scatter_dimension=2, tiled=True)
    router_grad = lax.psum(columns, "expert")
    prob_total, square_total = lax.psum(
        (jnp.stack(prob_sums), jnp.stack(square_sums)), ("dp", "expert")
    )
    share_table = jnp.stack(count_list) / (tokens_all * picks)
    balance = experts * jnp.sum(share_table * prob_total / tokens_all, axis=1)
    zloss = square_total / tokens_all
    return (router_grad, jnp.stack([balance, zloss], axis=-1))


def solution(mesh):
    in_specs = (P(None, ("dp", "expert"), None), P(), P(None, ("dp", "expert"), None))
    out_specs = (P(None, None, "dp"), P())
    return jax.shard_map(
        on_device, mesh=mesh, in_specs=in_specs, out_specs=out_specs, check_vma=False
    )
```

profile of v0, /device:TPU:0, one launch (start us, length us, event | category | flops | bytes accessed | tf_op | source)
XLA Modules:
  0.0 158.2 jit_solution(140643967143512886)
XLA Ops:
  7.2 2.3 %fusion.65 = (f32[256]{0:T(256)S(1)}, f32[8,256]{1,0:T(8,128)S(1)}) fusion(bf16[4,256,4096]{2,1,0:T(8,128)(2,1)} %param.3, bf16[4,8,4096]{2,1,0:T(8,128)(2,1)} %param.4), kind=kOutput, calls=%fused_computation.112 | convolution fusion | flops 16779008 | bytes 2171904 | tf_op jit(solution)/shard_map/dot_general | solution.py:30
  9.5 2.3 %fusion.66 = (f32[256]{0:T(256)S(1)}, f32[8,256]{1,0:T(8,128)S(1)}) fusion(bf16[4,256,4096]{2,1,0:T(8,128)(2,1)} %param.3, bf16[4,8,4096]{2,1,0:T(8,128)(2,1)} %param.4), kind=kOutput, calls=%fused_computation.113 | convolution fusion | flops 16779008 | bytes 2171904 | tf_op jit(solution)/shard_map/dot_general | solution.py:30
  11.8 2.3 %fusion.63 = (f32[256]{0:T(256)S(1)}, f32[8,256]{1,0:T(8,128)S(1)}) fusion(bf16[4,256,4096]{2,1,0:T(8,128)(2,1)} %param.3, bf16[4,8,4096]{2,1,0:T(8,128)(2,1)} %param.4), kind=kOutput, calls=%fused_computation.110 | convolution fusion | flops 16779008 | bytes 2171904 | tf_op jit(solution)/shard_map/dot_general | solution.py:30
  14.1 0.7 slice_bitcast_fusion.3
  14.9 0.1 convert_reduce_fusion.6
  15.9 2.3 %fusion.64 = (f32[256]{0:T(256)S(1)}, f32[8,256]{1,0:T(8,128)S(1)}) fusion(bf16[4,256,4096]{2,1,0:T(8,128)(2,1)} %param.3, bf16[4,8,4096]{2,1,0:T(8,128)(2,1)} %param.4), kind=kOutput, calls=%fused_computation.111 | convolution fusion | flops 16779008 | bytes 2171904 | tf_op jit(solution)/shard_map/dot_general | solution.py:30
  18.2 42.0 %all-reduce.1 = (f32[8]{0:T(128)S(1)}, f32[8]{0:T(128)S(1)}, f32[8]{0:T(128)S(1)}, f32[8]{0:T(128)S(1)}) all-reduce(f32[8]{0:T(128)S(1)} %add.46, f32[8]{0:T(128)S(1)} %add.44, f32[8]{0:T(128)S(1)} %add.42, f32[8]{0:T(128)S(1)} %add.40), channel_id=1, replica_groups=mesh['dp'=8,'expert'=4] {'dp','expert'}, use_global_device_ids=true, to_apply=%region_18.0 | all-reduce | flops 32 | bytes 256 | tf_op jit(solution)/shard_map/psum | solution.py:42
  60.2 0.6 multiply_reduce_fusion.6
  60.8 0.7 multiply_reduce_fusion.7
  61.5 0.6 multiply_reduce_fusion.4
  62.1 0.6 multiply_reduce_fusion.5
  62.7 0.2 fusion.55
  62.9 2.0 %convolution_bitcast_fusion.3 = f32[1,8,4096]{2,1,0:T(8,128)S(1)} fusion(bf16[4,256,4096]{2,1,0:T(8,128)(2,1)} %param.3, f32[256]{0:T(256)S(1)} %get-tuple-element.29, f32[256]{0:T(256)S(1)} %get-tuple-element.3, f32[8]{0:T(128)S(1)} %broadcast_multiply_fusion.3, f32[8,256]{1,0:T(8,128)S(1)} %get-tuple-element.43, f32[256]{0:T(256)S(1)} %get-tuple-element.42), kind=kOutput, calls=%fused_computation.3 | convolution fusion | flops 16787456 | bytes 2239520 | tf_op jit(solution)/shard_map/dot_general | solution.py:49
  64.9 2.0 %convolution_bitcast_fusion.2 = f32[1,8,4096]{2,1,0:T(8,128)S(1)} fusion(bf16[4,256,4096]{2,1,0:T(8,128)(2,1)} %param.3, f32[256]{0:T(256)S(1)} %get-tuple-element.31, f32[256]{0:T(256)S(1)} %get-tuple-element.44, f32[8]{0:T(128)S(1)} %broadcast_multiply_fusion.2, f32[8,256]{1,0:T(8,128)S(1)} %get-tuple-element.41, f32[256]{0:T(256)S(1)} %get-tuple-element.40), kind=kOutput, calls=%fused_computation.2 | convolution fusion | flops 16787456 | bytes 2239520 | tf_op jit(solution)/shard_map/dot_general | solution.py:49
  66.9 0.2 fusion.57
  67.1 2.0 %convolution_bitcast_fusion.1 = f32[1,8,4096]{2,1,0:T(8,128)S(1)} fusion(bf16[4,256,4096]{2,1,0:T(8,128)(2,1)} %param.3, f32[256]{0:T(256)S(1)} %get-tuple-element.33, f32[256]{0:T(256)S(1)} %get-tuple-element.7, f32[8]{0:T(128)S(1)} %broadcast_multiply_fusion.1, f32[8,256]{1,0:T(8,128)S(1)} %get-tuple-element.39, f32[256]{0:T(256)S(1)} %get-tuple-element.38), kind=kOutput, calls=%fused_computation.1 | convolution fusion | flops 16787456 | bytes 2239520 | tf_op jit(solution)/shard_map/dot_general | solution.py:49
  69.1 2.0 %convolution_bitcast_fusion = f32[1,8,4096]{2,1,0:T(8,128)S(1)} fusion(bf16[4,256,4096]{2,1,0:T(8,128)(2,1)} %param.3, f32[256]{0:T(256)S(1)} %get-tuple-element.35, f32[256]{0:T(256)S(1)} %get-tuple-element.46, f32[8]{0:T(128)S(1)} %broadcast_multiply_fusion, f32[8,256]{1,0:T(8,128)S(1)} %get-tuple-element.37, f32[256]{0:T(256)S(1)} %get-tuple-element.36), kind=kOutput, calls=%fused_computation | convolution fusion | flops 16787456 | bytes 2239520 | tf_op jit(solution)/shard_map/dot_general | solution.py:49
  71.1 0.8 pad_maximum_fusion
  72.0 2.6 %pad_maximum_fusion.3 = f32[4]{0:T(128)S(1)} fusion(f32[1]{0:T(128)} %bitcast.36, f32[1]{0:T(128)} %bitcast.35, f32[1]{0:T(128)} %bitcast.34, f32[1]{0:T(128)} %bitcast.33), kind=kLoop, calls=%fused_computation.95 | loop fusion | flops 12 | bytes 32 | tf_op jit(solution)/shard_map/stack | solution.py:54
  74.6 40.0 %all-reduce = (f32[4]{0:T(128)S(1)}, f32[4,8]{1,0:T(4,128)S(1)}) all-reduce(f32[4]{0:T(128)S(1)} %pad_maximum_fusion.3, f32[4,8]{1,0:T(4,128)S(1)} %pad_maximum_fusion.1), channel_id=1, replica_groups=mesh['dp'=8,'expert'=4] {'dp','expert'}, use_global_device_ids=true, to_apply=%region_32.0 | all-reduce | flops 36 | bytes 288 | tf_op jit(solution)/shard_map/psum | solution.py:53
  114.7 0.1 fusion.54
  114.8 0.6 pad_maximum_fusion.2
  115.4 34.5 %all-reduce.4.cloned.1.call-done = f32[4,8,512]{2,1,0:T(8,128)} async-done(((f32[4,8,512]{2,1,0:T(8,128)}), f32[4,8,512]{2,1,0:T(8,128)}) %all-reduce.4.cloned.1.call-update) | async-done | bytes 65552 | tf_op jit(solution)/shard_map/psum | solution.py:52
  149.9 1.5 copy.6
  (27 shorter events, 1.0 us)
Async XLA Ops:
  7.2 107.6 %reduce-scatter.2.cloned.1.call-start = ((), (), s32[]{:S(2)}) async-start(), calls=%async_computation.1 | async-start | bytes 589824 | tf_op jit(solution)/shard_map/reduce_scatter | solution.py:51
  71.9 78.0 %all-reduce.4.cloned.1.call-start = ((), (), s32[]{:S(2)}) async-start(), calls=%async_computation.2 | async-start | bytes 131072 | tf_op jit(solution)/shard_map/psum | solution.py:52
Sparse Core Ops, SparseCore 0:
  72.1 33.9 reduce-scatter.1
  115.0 34.9 all-reduce.3
where the time goes:
time: 159 us; the launch traced here: 158 us
  blocking collectives  82.1 us (52%)
  waiting for transfers between devices  34.6 us (22%)
  matrix products  17.3 us (11%)
  between operations  14.2 us (9%)
  other arithmetic  7.88 us (5%)
  local copies, waits for them, and re-layouts  2.23 us (1%)
    psum x1, blocking collectives, on_device(): lax.psum(local_counts(expert_ids[layer], experts), ('dp', 'expert'))  42 us
    psum x1, blocking collectives, on_device(): lax.psum((jnp.stack(prob_sums), jnp.stack(square_sums)), ('dp', 'expert'))  40 us
    psum x1, waiting for transfers between devices, on_device(): router_grad = lax.psum(columns, 'expert')  34.5 us
    dot_general x4, matrix products, on_device(): lax.dot_general(router_weight[layer], states, (((1,), (1,)), ((), ())), p...  9.21 us
    dot_general x4, matrix products, on_device(): term = jnp.dot(dlogits, states, preferred_element_type=jnp.float32)  8.06 us
  transfers between devices with their start and end apart: 2, of which 1 were waited for; matrix products, arithmetic and copies ran while one was open for 2% of the time, Pallas kernels for 0%

commit v1 on v0

--- a/solution.py
+++ b/solution.py
@@ -5,6 +5,11 @@
 
 balance_coef = 0.02
 zloss_coef = 0.001
+
+
+def gather_and_add(x, axis):
+    terms = lax.all_gather(x, axis)
+    return jnp.sum(terms, axis=0)
 
 
 def local_counts(chosen, experts):
@@ -49,7 +54,7 @@
         term = jnp.dot(dlogits, states, preferred_element_type=jnp.float32)
         terms.append(term)
     columns = lax.psum_scatter(jnp.stack(terms), "dp", scatter_dimension=2, tiled=True)
-    router_grad = lax.psum(columns, "expert")
+    router_grad = gather_and_add(columns, "expert")
     prob_total, square_total = lax.psum(
         (jnp.stack(prob_sums), jnp.stack(square_sums)), ("dp", "expert")
     )

time: 159 us -> 138 us (0.87)
  waiting for transfers between devices: 34.6 us -> 0.02 us
  blocking collectives: 82.1 us -> 96.7 us
    psum x1 -> x0, waiting for transfers between devices: 34.5 us -> none  [on_device(): router_grad = lax.psum(columns, 'expert')]
    all_gather x0 -> x1, blocking collectives: none -> 14.6 us  [gather_and_add(): terms = lax.all_gather(x, axis)]
  transfers between devices with their start and end apart: 2 -> 1, of which waited for: 1 -> 0; matrix products, arithmetic and copies ran while one was open for 2% -> 2% of each run, Pallas kernels for 0% -> 0%
where the time goes in v1:
time: 138 us; the launch traced here: 137 us
  blocking collectives  96.7 us (70%)
  matrix products  17.3 us (13%)
  between operations  14.1 us (10%)
  other arithmetic  8.53 us (6%)
    psum x1, blocking collectives, on_device(): lax.psum(local_counts(expert_ids[layer], experts), ('dp', 'expert'))  42 us
    psum x1, blocking collectives, on_device(): lax.psum((jnp.stack(prob_sums), jnp.stack(square_sums)), ('dp', 'expert'))  40 us
    all_gather x1, blocking collectives, gather_and_add(): terms = lax.all_gather(x, axis)  14.6 us
    dot_general x4, matrix products, on_device(): lax.dot_general(router_weight[layer], states, (((1,), (1,)), ((), ())), p...  9.21 us
    dot_general x4, matrix products, on_device(): term = jnp.dot(dlogits, states, preferred_element_type=jnp.float32)  8.06 us
  transfers between devices with their start and end apart: 1, of which 0 were waited for; matrix products, arithmetic and copies ran while one was open for 2% of the time, Pallas kernels for 0%

profile of v1, /device:TPU:0, one launch (start us, length us, event | category | flops | bytes accessed | tf_op | source)
XLA Modules:
  0.0 137.4 jit_solution(5159721153701160064)
XLA Ops:
  7.2 2.3 %fusion.65 = (f32[256]{0:T(256)S(1)}, f32[8,256]{1,0:T(8,128)S(1)}) fusion(bf16[4,256,4096]{2,1,0:T(8,128)(2,1)} %param.3, bf16[4,8,4096]{2,1,0:T(8,128)(2,1)} %param.4), kind=kOutput, calls=%fused_computation.112 | convolution fusion | flops 16779008 | bytes 2171904 | tf_op jit(solution)/shard_map/dot_general | solution.py:35
  9.5 2.3 %fusion.66 = (f32[256]{0:T(256)S(1)}, f32[8,256]{1,0:T(8,128)S(1)}) fusion(bf16[4,256,4096]{2,1,0:T(8,128)(2,1)} %param.3, bf16[4,8,4096]{2,1,0:T(8,128)(2,1)} %param.4), kind=kOutput, calls=%fused_computation.113 | convolution fusion | flops 16779008 | bytes 2171904 | tf_op jit(solution)/shard_map/dot_general | solution.py:35
  11.8 2.3 %fusion.63 = (f32[256]{0:T(256)S(1)}, f32[8,256]{1,0:T(8,128)S(1)}) fusion(bf16[4,256,4096]{2,1,0:T(8,128)(2,1)} %param.3, bf16[4,8,4096]{2,1,0:T(8,128)(2,1)} %param.4), kind=kOutput, calls=%fused_computation.110 | convolution fusion | flops 16779008 | bytes 2171904 | tf_op jit(solution)/shard_map/dot_general | solution.py:35
  14.1 0.7 slice_bitcast_fusion.3
  14.9 0.1 convert_reduce_fusion.6
  15.9 2.3 %fusion.64 = (f32[256]{0:T(256)S(1)}, f32[8,256]{1,0:T(8,128)S(1)}) fusion(bf16[4,256,4096]{2,1,0:T(8,128)(2,1)} %param.3, bf16[4,8,4096]{2,1,0:T(8,128)(2,1)} %param.4), kind=kOutput, calls=%fused_computation.111 | convolution fusion | flops 16779008 | bytes 2171904 | tf_op jit(solution)/shard_map/dot_general | solution.py:35
  18.2 42.0 %all-reduce.1 = (f32[8]{0:T(128)S(1)}, f32[8]{0:T(128)S(1)}, f32[8]{0:T(128)S(1)}, f32[8]{0:T(128)S(1)}) all-reduce(f32[8]{0:T(128)S(1)} %add.44, f32[8]{0:T(128)S(1)} %add.42, f32[8]{0:T(128)S(1)} %add.40, f32[8]{0:T(128)S(1)} %add.38), channel_id=1, replica_groups=mesh['dp'=8,'expert'=4] {'dp','expert'}, use_global_device_ids=true, to_apply=%region_18.0 | all-reduce | flops 32 | bytes 256 | tf_op jit(solution)/shard_map/psum | solution.py:47
  60.2 0.6 multiply_reduce_fusion.6
  60.8 0.7 multiply_reduce_fusion.7
  61.5 0.6 multiply_reduce_fusion.4
  62.1 0.6 multiply_reduce_fusion.5
  62.7 0.2 fusion.55
  62.9 2.0 %convolution_bitcast_fusion.3 = f32[1,8,4096]{2,1,0:T(8,128)S(1)} fusion(bf16[4,256,4096]{2,1,0:T(8,128)(2,1)} %param.3, f32[256]{0:T(256)S(1)} %get-tuple-element.29, f32[256]{0:T(256)S(1)} %get-tuple-element.3, f32[8]{0:T(128)S(1)} %broadcast_multiply_fusion.3, f32[8,256]{1,0:T(8,128)S(1)} %get-tuple-element.43, f32[256]{0:T(256)S(1)} %get-tuple-element.42), kind=kOutput, calls=%fused_computation.3 | convolution fusion | flops 16787456 | bytes 2239520 | tf_op jit(solution)/shard_map/dot_general | solution.py:54
  64.9 2.0 %convolution_bitcast_fusion.2 = f32[1,8,4096]{2,1,0:T(8,128)S(1)} fusion(bf16[4,256,4096]{2,1,0:T(8,128)(2,1)} %param.3, f32[256]{0:T(256)S(1)} %get-tuple-element.31, f32[256]{0:T(256)S(1)} %get-tuple-element.44, f32[8]{0:T(128)S(1)} %broadcast_multiply_fusion.2, f32[8,256]{1,0:T(8,128)S(1)} %get-tuple-element.41, f32[256]{0:T(256)S(1)} %get-tuple-element.40), kind=kOutput, calls=%fused_computation.2 | convolution fusion | flops 16787456 | bytes 2239520 | tf_op jit(solution)/shard_map/dot_general | solution.py:54
  66.9 0.2 fusion.57
  67.0 2.0 %convolution_bitcast_fusion.1 = f32[1,8,4096]{2,1,0:T(8,128)S(1)} fusion(bf16[4,256,4096]{2,1,0:T(8,128)(2,1)} %param.3, f32[256]{0:T(256)S(1)} %get-tuple-element.33, f32[256]{0:T(256)S(1)} %get-tuple-element.7, f32[8]{0:T(128)S(1)} %broadcast_multiply_fusion.1, f32[8,256]{1,0:T(8,128)S(1)} %get-tuple-element.39, f32[256]{0:T(256)S(1)} %get-tuple-element.38), kind=kOutput, calls=%fused_computation.1 | convolution fusion | flops 16787456 | bytes 2239520 | tf_op jit(solution)/shard_map/dot_general | solution.py:54
  69.1 2.0 %convolution_bitcast_fusion = f32[1,8,4096]{2,1,0:T(8,128)S(1)} fusion(bf16[4,256,4096]{2,1,0:T(8,128)(2,1)} %param.3, f32[256]{0:T(256)S(1)} %get-tuple-element.35, f32[256]{0:T(256)S(1)} %get-tuple-element.46, f32[8]{0:T(128)S(1)} %broadcast_multiply_fusion, f32[8,256]{1,0:T(8,128)S(1)} %get-tuple-element.37, f32[256]{0:T(256)S(1)} %get-tuple-element.36), kind=kOutput, calls=%fused_computation | convolution fusion | flops 16787456 | bytes 2239520 | tf_op jit(solution)/shard_map/dot_general | solution.py:54
  71.1 0.8 pad_maximum_fusion
  71.9 2.6 %pad_maximum_fusion.3 = f32[4]{0:T(128)S(1)} fusion(f32[1]{0:T(128)} %bitcast.37, f32[1]{0:T(128)} %bitcast.36, f32[1]{0:T(128)} %bitcast.35, f32[1]{0:T(128)} %bitcast.34), kind=kLoop, calls=%fused_computation.95 | loop fusion | flops 12 | bytes 32 | tf_op jit(solution)/shard_map/stack | solution.py:59
  74.5 40.0 %all-reduce = (f32[4]{0:T(128)S(1)}, f32[4,8]{1,0:T(4,128)S(1)}) all-reduce(f32[4]{0:T(128)S(1)} %pad_maximum_fusion.3, f32[4,8]{1,0:T(4,128)S(1)} %pad_maximum_fusion.1), channel_id=1, replica_groups=mesh['dp'=8,'expert'=4] {'dp','expert'}, use_global_device_ids=true, to_apply=%region_32.0 | all-reduce | flops 36 | bytes 288 | tf_op jit(solution)/shard_map/psum | solution.py:58
  114.6 0.1 fusion.54
  114.7 0.6 pad_maximum_fusion.2
  115.3 14.6 %all-gather = f32[16,8,512]{2,1,0:T(8,128)S(1)} all-gather(f32[4,8,512]{2,1,0:T(8,128)} %reduce-scatter.2.cloned.1.call-done), channel_id=2, replica_groups=mesh['dp'=8,'expert'=4] {'expert'}, dimensions={0}, use_global_device_ids=true | all-gather | bytes 327680 | tf_op jit(solution)/shard_map/all_gather | solution.py:11
  129.9 0.6 reduce_sum.250
  (25 shorter events, 0.9 us)
Async XLA Ops:
  7.2 108.1 %reduce-scatter.2.cloned.1.call-start = ((), (), s32[]{:S(2)}) async-start(), calls=%async_computation.1 | async-start | bytes 589824 | tf_op jit(solution)/shard_map/reduce_scatter | solution.py:56
Sparse Core Ops, SparseCore 0:
  72.0 33.9 reduce-scatter.1
